TPU v7x, 256 devices: a whole 4x4x8 slice. The times are simulated.
256 devices in a mesh: dp: 8 (over z), vocab: 32 (over x, y, core).
Axes of the slice: x: 4, y: 4, z: 8, core: 2. Of those that a mesh axis runs over, the one named last changes fastest.
Arguments:
- hidden: bfloat16 [8, 2, 64, 4608], P('dp'), may hold values from -6 to 6
- table: bfloat16 [73728, 4608], P('vocab', 'dp'), may hold values from -0.25 to 0.25
- new_mask: int32 [73728], P('vocab'), may hold values from 0 to 1, as said below
- labels: int32 [8, 2, 64], P('dp'), may hold values from 0 to 73727
- in_grad: bfloat16 [8, 2, 768, 4608], P('dp', None, 'vocab'), may hold values from -0.75 to 0.75
- item_owner: int32 [8, 2, 768, 1], P('dp', None, 'vocab'), may hold values from 0 to 31; in each aligned block of 24 rows (0 to 23, 24 to 47, ..., all dimensions but the last counted through in order) at most 2 rows name the same one
- item_slot: int32 [8, 2, 768], P('dp', None, 'vocab'), may hold values from 0 to 255
- first_moment: float32 [8192, 4608], P('vocab', 'dp'), may hold values from -0.75 to 0.75
- second_moment: float32 [8192, 4608], P('vocab', 'dp'), may hold values from 0.0001 to 0.01
Outputs:
- token_loss: float32 [8, 2, 64], P('dp')
- d_hidden: bfloat16 [8, 2, 64, 4608], P('dp', None, None, 'vocab')
- update: float32 [8192, 4608], P('vocab', 'dp')
- first_out: float32 [8192, 4608], P('vocab', 'dp')
- second_out: float32 [8192, 4608], P('vocab', 'dp')
Inputs may be any that keep to these rules, and one draw needn't show every extreme that they name: `new_mask`: each aligned block of 2304 entries holds exactly 256 ones. `item_owner`: within the 24 rows of one device in one block, no shard is named more than 2 times, a bound that some block reaches.
All inputs are finite; a program needn't handle non-finite values.
Results may differ from a plain program's by a relative error of at most 0.006.
Values may be sent and summed in bfloat16 or wider, within the bound.
No kernel may reach another device: no remote copies, remote signals or barrier semaphores. Data moves between devices by JAX's collectives and lax.ppermute only.
A program may use at most 128 MiB of HBM per device.

v0:
```python
import jax
import jax.numpy as jnp
from jax import lax
from jax.sharding import PartitionSpec as P

cap_value = 30.0
beta_one = 0.9
beta_two = 0.95
step_count = 10
epsilon = 1e-08
decay_rate = 0.1


def sent_to_all(array, axis):
    peers = lax.axis_size(axis)
    return lax.all_to_all(
        jnp.broadcast_to(array[None], (peers, *array.shape)), axis, 0, 0, tiled=True
    )


def over_copies(array, axis):
    return sent_to_all(array, axis).sum(axis=0)


def packed_total(arrays, axis):
    line, at, gathered = (jnp.concatenate([a.reshape(-1) for a in arrays]), 0, [])
    subtotal = over_copies(line, axis)
    for a in arrays:
        gathered.append(subtotal[at : at + a.size].reshape(a.shape))
        at += a.size
    return tuple(gathered)


def in_blocks(array, dim, peers):
    shape = array.shape
    parts = array.reshape(*shape[:dim], peers, shape[dim] // peers, *shape[dim + 1 :])
    return jnp.moveaxis(parts, dim, 0)


def sent_and_summed(array, axis, dim):
    parts = in_blocks(array, dim, lax.axis_size(axis))
    arrived = lax.all_to_all(parts, axis, split_axis=0, concat_axis=0, tiled=True)
    return arrived.sum(axis=0)


def select_rows(new_mask, new_count):
    ranked = jnp.cumsum(new_mask) - 1
    wanted = (ranked[None, :] == jnp.arange(new_count, dtype=jnp.int32)[:, None]) & (
        new_mask[None, :] == 1
    )
    return wanted.astype(jnp.bfloat16)


def softmax_error(raw, label_row, vocab_start):
    capped = cap_value * jnp.tanh(raw / cap_value)
    expd = jnp.exp(capped)
    hits = jnp.arange(raw.shape[1], dtype=jnp.int32)[None, :] + vocab_start == label_row[:, None]
    local_total = jnp.sum(expd, axis=1)
    local_pick = jnp.sum(jnp.where(hits, capped, 0.0), axis=1)
    total, picked = packed_total((local_total, local_pick), "vocab")
    loss = jnp.log(total) - picked
    error = (
        (expd / total[:, None] - hits.astype(jnp.float32)) * (1.0 - (capped / cap_value) ** 2)
    ).astype(jnp.bfloat16)
    return (loss, error)


def finish_hidden(partial_value):
    return sent_and_summed(partial_value, "vocab", 1).astype(jnp.bfloat16)


def pack_items(rows, owner, slot, shards, capacity):
    onehot = (owner[:, None] == jnp.arange(shards, dtype=jnp.int32)[None, :]).astype(jnp.int32)
    running = jnp.cumsum(onehot, axis=0)
    ranked = jnp.sum(onehot * running, axis=1) - 1
    place = owner * capacity + ranked
    placing = jnp.arange(shards * capacity, dtype=jnp.int32)[:, None] == place[None, :]
    sent = jnp.dot(placing.astype(jnp.bfloat16), rows, preferred_element_type=jnp.float32).astype(
        jnp.bfloat16
    )
    targets = jnp.sum(placing.astype(jnp.int32) * (slot + 1)[None, :], axis=1) - 1
    return (sent.reshape(shards, capacity, rows.shape[1]), targets.reshape(shards, capacity))


def scatter_items(rows, targets, new_count):
    picking = (jnp.arange(new_count, dtype=jnp.int32)[:, None] == targets[None, :]).astype(
        jnp.bfloat16
    )
    return jnp.dot(picking, rows, preferred_element_type=jnp.float32)


def body(
    hidden, table, new_mask, labels, in_grad, item_owner, item_slot, first_moment, second_moment
):
    blocks = hidden.shape[1]
    width = hidden.shape[3]
    new_count = first_moment.shape[0]
    shards = lax.axis_size("vocab")
    items_here = in_grad.shape[2]
    capacity = max(2, (2 * items_here + shards - 1) // shards)
    vocab_start = lax.axis_index("vocab") * table.shape[0]
    select = select_rows(new_mask, new_count)
    params = jnp.dot(select, table, preferred_element_type=jnp.float32)
    received_rows = []
    received_targets = []
    losses = []
    dstates = []
    full_table = lax.all_gather(table, "dp", axis=1, tiled=True)
    grads = jnp.zeros((new_count, width), jnp.float32)
    for c in range(blocks):
        states = hidden[0, c]
        raw = lax.dot_general(
            states, full_table, (((1,), (1,)), ((), ())), preferred_element_type=jnp.float32
        )
        loss, error = softmax_error(raw, labels[0, c], vocab_start)
        partial_value = jnp.dot(error, full_table, preferred_element_type=jnp.float32)
        dstates.append(finish_hidden(partial_value))
        chosen = lax.dot_general(
            error, select, (((1,), (1,)), ((), ())), preferred_element_type=jnp.float32
        ).astype(jnp.bfloat16)
        grads = grads + lax.dot_general(
            chosen, states, (((0,), (0,)), ((), ())), preferred_element_type=jnp.float32
        )
        losses.append(loss)
        sent_rows, sent_targets = pack_items(
            in_grad[0, c], item_owner[0, c, :, 0], item_slot[0, c], shards, capacity
        )
        got_rows, got_targets = (
            lax.all_to_all(sent_rows, "vocab", split_axis=0, concat_axis=0, tiled=True),
            lax.all_to_all(sent_targets, "vocab", split_axis=0, concat_axis=0, tiled=True),
        )
        received_rows.append(got_rows.reshape(-1, width))
        received_targets.append(got_targets.reshape(-1))
    item_rows = jnp.concatenate(received_rows, axis=0)
    item_targets = jnp.concatenate(received_targets, axis=0)
    grads = grads + scatter_items(item_rows, item_targets, new_count)
    grads = lax.psum_scatter(grads, "dp", scatter_dimension=1, tiled=True)
    first_out = beta_one * first_moment + (1.0 - beta_one) * grads
    second_out = beta_two * second_moment + (1.0 - beta_two) * grads * grads
    update = (
        first_out
        / (1.0 - beta_one**step_count)
        / (jnp.sqrt(second_out / (1.0 - beta_two**step_count)) + epsilon)
        + decay_rate * params
    )
    token_loss = jnp.stack(losses)[None]
    d_hidden = jnp.stack(dstates)[None]
    return (token_loss, d_hidden, update, first_out, second_out)


def solution(mesh):
    return jax.shard_map(
        body,
        mesh=mesh,
        in_specs=(
            P("dp", None, None, None),
            P("vocab", "dp"),
            P("vocab"),
            P("dp", None, None),
            P("dp", None, "vocab", None),
            P("dp", None, "vocab", None),
            P("dp", None, "vocab"),
            P("vocab", "dp"),
            P("vocab", "dp"),
        ),
        out_specs=(
            P("dp", None, None),
            P("dp", None, None, "vocab"),
            P("vocab", "dp"),
            P("vocab", "dp"),
            P("vocab", "dp"),
        ),
        check_vma=False,
    )
```

profile of v0, /device:TPU:1, one launch (start us, length us, event | category | flops | bytes accessed | tf_op | source)
XLA Modules:
  0.0 393.1 jit_solution(2182474801881133417)
XLA Ops:
  7.2 0.0 all-gather.2.cloned.1.call-start
  7.3 0.7 all-gather.2.cloned.1.call-update
  8.0 0.1 fusion.58
  8.1 0.1 fusion.57
  8.2 0.2 select_reduce_fusion.1
  8.4 0.1 select_reduce_fusion
  8.5 0.7 sub.53
  9.2 8.6 %all-to-all-start.5 = ((s32[32,1,2]{2,1,0:T(1,128)}), s32[32,1,2]{2,1,0:T(1,128)S(1)}, u32[]{:S(2)}, u32[]{:S(2)}) async-start(s32[32,1,2]{2,1,0:T(1,128)} %bitcast.21), calls=%async_computation.5 | async-start | bytes 32768 | tf_op jit(solution)/shard_map/all_to_all | solution.py:130
  17.8 0.3 reduce-window.9
  18.1 0.1 slice.65
  18.2 0.1 slice_reduce_fusion
  18.4 0.1 select_reduce_fusion.2
  18.5 0.1 add_bitcast_fusion
  18.6 0.4 convolution_convert_fusion
  19.0 0.4 convolution_convert_fusion.1
  19.5 0.7 sub.50
  20.2 4.6 %all-to-all-done.5 = s32[32,1,2]{2,1,0:T(1,128)S(1)} async-done(((s32[32,1,2]{2,1,0:T(1,128)}), s32[32,1,2]{2,1,0:T(1,128)S(1)}, u32[]{:S(2)}, u32[]{:S(2)}) %all-to-all-start.5) | async-done | bytes 288 | tf_op jit(solution)/shard_map/all_to_all | solution.py:130
  24.7 4.1 %all-to-all-start.4 = ((s32[32,1,2]{2,1,0:T(1,128)}), s32[32,1,2]{2,1,0:T(1,128)S(1)}, u32[]{:S(2)}, u32[]{:S(2)}) async-start(s32[32,1,2]{2,1,0:T(1,128)} %bitcast.18), calls=%async_computation.4 | async-start | bytes 32768 | tf_op jit(solution)/shard_map/all_to_all | solution.py:130
  28.9 1.0 reshape.176
  29.9 1.0 reshape.174
  30.9 0.5 broadcast.174
  31.5 0.7 reduce.10
  32.2 0.1 reshape.173
  32.3 3.6 all-to-all-done.4
  35.9 4.2 %all-to-all-start.7 = ((bf16[32,2,4608]{2,1,0:T(2,128)(2,1)}), bf16[32,2,4608]{2,1,0:T(2,128)(2,1)S(1)}, u32[]{:S(2)}, u32[]{:S(2)}) async-start(bf16[32,2,4608]{2,1,0:T(2,128)(2,1)} %reshape.176), calls=%async_computation.7 | async-start | bytes 1179648 | tf_op jit(solution)/shard_map/all_to_all | solution.py:129
  40.1 0.7 reduce.11
  40.8 0.1 reshape.172
  40.9 187.1 %all-gather.2.cloned.1.call-done = bf16[2304,4608]{0,1:T(8,128)(2,1)} async-done(((bf16[2304,576]{0,1:T(8,128)(2,1)}), bf16[2304,4608]{0,1:T(8,128)(2,1)}) %all-gather.2.cloned.1.call-update) | async-done | bytes 21233680 | tf_op jit(solution)/shard_map/all_gather | solution.py:108
  228.0 9.1 %fusion.1 = f32[64,2304]{1,0:T(8,128)S(1)} fusion(bf16[2304,4608]{0,1:T(8,128)(2,1)} %all-gather.2.cloned.1.call-done, bf16[1,2,64,4608]{3,2,1,0:T(8,128)(2,1)S(1)} %copy-done), kind=kOutput, calls=%fused_computation.7 | convolution fusion | flops 1359101952 | bytes 22413312 | tf_op jit(solution)/shard_map/dot_general | solution.py:112
  237.1 7.8 %all-to-all-start.6 = ((bf16[32,2,4608]{2,1,0:T(2,128)(2,1)}), bf16[32,2,4608]{2,1,0:T(2,128)(2,1)}, u32[]{:S(2)}, u32[]{:S(2)}) async-start(bf16[32,2,4608]{2,1,0:T(2,128)(2,1)} %reshape.174), calls=%async_computation.6 | async-start | bytes 1179648 | tf_op jit(solution)/shard_map/all_to_all | solution.py:129
  244.9 9.2 %exponential_reduce_fusion.1 = (f32[64]{0:T(128)S(1)}, f32[64]{0:T(128)S(1)}, f32[64]{0:T(128)S(1)}, f32[64]{0:T(128)S(1)}, f32[64,2304]{1,0:T(8,128)S(1)}) fusion(s32[64]{0:T(128)S(1)} %get-tuple-element.19, s32[2304]{0:T(1024)S(1)} %iota_add_fusion, s32[64]{0:T(128)S(1)} %get-tuple-element.20, f32[64,2304]{1,0:T(8,128)S(1)} %fusion.1, ...), kind=kOutput, calls=%fused_computation.49 | convolution fusion | flops 1360576512 | bytes 23017472 | tf_op jit(solution)/shard_map/dot_general | solution.py:112
  254.1 0.1 pad_maximum_fusion.1
  254.2 3.0 all-to-all-done.6
  257.2 0.6 broadcast_in_dim.15
  257.8 4.4 %all-to-all-start.1 = ((f32[32,1,128]{2,1,0:T(1,128)}), f32[32,1,128]{2,1,0:T(1,128)S(1)}, u32[]{:S(2)}, u32[]{:S(2)}) async-start(f32[32,1,128]{2,1,0:T(1,128)} %broadcast_in_dim.15), calls=%async_computation.1 | async-start | bytes 32768 | tf_op jit(solution)/shard_map/all_to_all | solution.py:16
  262.2 0.1 pad_maximum_fusion
  262.3 6.8 %all-to-all-done.1 = f32[32,1,128]{2,1,0:T(1,128)S(1)} async-done(((f32[32,1,128]{2,1,0:T(1,128)}), f32[32,1,128]{2,1,0:T(1,128)S(1)}, u32[]{:S(2)}, u32[]{:S(2)}) %all-to-all-start.1) | async-done | bytes 16416 | tf_op jit(solution)/shard_map/all_to_all | solution.py:16
  269.1 0.6 broadcast_in_dim.14
  269.7 4.1 %all-to-all-start = ((f32[32,1,128]{2,1,0:T(1,128)}), f32[32,1,128]{2,1,0:T(1,128)S(1)}, u32[]{:S(2)}, u32[]{:S(2)}) async-start(f32[32,1,128]{2,1,0:T(1,128)} %broadcast_in_dim.14), calls=%async_computation | async-start | bytes 32768 | tf_op jit(solution)/shard_map/all_to_all | solution.py:16
  273.8 0.2 reduce-scatter.2.cloned.1.call-start
  274.1 0.1 pad_add_fusion
  274.2 1.0 reshape.177
  275.2 2.1 reshape.175
  277.3 3.5 all-to-all-done
  280.9 0.1 fusion.70
  281.0 4.1 %fusion.33 = f32[256,4608]{0,1:T(8,128)} fusion(s32[2304]{0:T(1024)S(1)} %add_bitcast_fusion, pred[2304]{0:T(1024)(128)(4,1)S(1)} %broadcast_compare_fusion, bf16[1,2,64,4608]{3,2,1,0:T(8,128)(2,1)S(1)} %copy-done, f32[64,2304]{1,0:T(8,128)S(1)} %get-tuple-element.25, f32[64]{0:T(128)S(1)} %get-tuple-element.21, s32[2304]{0:T(1024)S(1)} %iota_add_fusion, ...), kind=kOutput, calls=%fused_computation.28 | convolution fusion | flops 229015552 | bytes 5926912 | tf_op jit(solution)/shard_map/dot_general | solution.py:121
  285.0 6.5 %convolution_add_fusion.1 = f32[256,4608]{0,1:T(8,128)} fusion(f32[256,4608]{0,1:T(8,128)} %fusion.33, s32[2304]{0:T(1024)S(1)} %add_bitcast_fusion, pred[2304]{0:T(1024)(128)(4,1)S(1)} %broadcast_compare_fusion, bf16[1,2,64,4608]{3,2,1,0:T(8,128)(2,1)S(1)} %copy-done, f32[64,2304]{1,0:T(8,128)S(1)} %fusion.1, f32[64]{0:T(128)S(1)} %get-tuple-element.27, ...), kind=kOutput, calls=%fused_computation.1 | convolution fusion | flops 230195200 | bytes 10645504 | tf_op jit(solution)/shard_map/dot_general | solution.py:121
  291.5 5.5 %convolution_add_fusion = f32[256,4608]{0,1:T(8,128)} fusion(f32[256,4608]{0,1:T(8,128)} %convolution_add_fusion.1, bf16[64,4608]{1,0:T(8,128)(2,1)S(1)} %copy-done.2, bf16[64,4608]{1,0:T(8,128)(2,1)} %reshape.175, s32[128]{0:T(128)S(1)} %pad_add_fusion), kind=kOutput, calls=%fused_computation | convolution fusion | flops 305561600 | bytes 10617344 | tf_op jit(solution)/shard_map/dot_general | solution.py:89
  297.1 11.7 %fusion.64 = f32[64,4608]{1,0:T(8,128)} fusion(bf16[2304,4608]{0,1:T(8,128)(2,1)} %all-gather.2.cloned.1.call-done, f32[64,2304]{1,0:T(8,128)S(1)} %fusion.1, f32[64]{0:T(128)S(1)} %get-tuple-element.27, s32[2304]{0:T(1024)S(1)} %iota_add_fusion, s32[64]{0:T(128)S(1)} %get-tuple-element.20), kind=kOutput, calls=%fused_computation.96 | convolution fusion | flops 1360281600 | bytes 23012864 | tf_op jit(solution)/shard_map/dot_general | solution.py:116
  308.8 2.7 reshape.169
  311.6 2.5 copy.30
  314.1 4.3 %all-to-all-start.3 = ((f32[32,64,144]{2,1,0:T(8,128)}), f32[32,64,144]{2,1,0:T(8,128)S(1)}, u32[]{:S(2)}, u32[]{:S(2)}) async-start(f32[32,64,144]{2,1,0:T(8,128)} %bitcast.67), calls=%async_computation.3 | async-start | bytes 4194304 | tf_op jit(solution)/shard_map/all_to_all | solution.py:42
  318.4 11.9 %fusion.68 = f32[64,4608]{1,0:T(8,128)} fusion(bf16[2304,4608]{0,1:T(8,128)(2,1)} %all-gather.2.cloned.1.call-done, f32[64,2304]{1,0:T(8,128)S(1)} %get-tuple-element.25, f32[64]{0:T(128)S(1)} %get-tuple-element.21, s32[2304]{0:T(1024)S(1)} %iota_add_fusion, s32[64]{0:T(128)S(1)} %get-tuple-element.19), kind=kOutput, calls=%fused_computation.97 | convolution fusion | flops 1360281600 | bytes 23012864 | tf_op jit(solution)/shard_map/dot_general | solution.py:116
  330.3 3.6 reshape.168
  333.9 4.2 %copy.31 = f32[64,32,144]{2,0,1:T(8,128)} copy(f32[64,32,144]{2,1,0:T(8,128)} %reshape.168) | data formatting | bytes 2359296 | tf_op jit(solution)/shard_map/reshape | solution.py:36
  338.1 8.7 %all-to-all-done.3 = f32[32,64,144]{2,1,0:T(8,128)S(1)} async-done(((f32[32,64,144]{2,1,0:T(8,128)}), f32[32,64,144]{2,1,0:T(8,128)S(1)}, u32[]{:S(2)}, u32[]{:S(2)}) %all-to-all-start.3) | async-done | bytes 1179680 | tf_op jit(solution)/shard_map/all_to_all | solution.py:42
  346.9 5.2 %all-to-all-start.2 = ((f32[32,64,144]{2,1,0:T(8,128)}), f32[32,64,144]{2,1,0:T(8,128)}, u32[]{:S(2)}, u32[]{:S(2)}) async-start(f32[32,64,144]{2,1,0:T(8,128)} %bitcast.66), calls=%async_computation.2 | async-start | bytes 4194304 | tf_op jit(solution)/shard_map/all_to_all | solution.py:42
  352.1 0.6 maximum_bitcast_fusion.1
  352.6 0.1 reduce_sum.115
  352.8 27.7 %all-to-all-done.2 = f32[32,64,144]{2,1,0:T(8,128)} async-done(((f32[32,64,144]{2,1,0:T(8,128)}), f32[32,64,144]{2,1,0:T(8,128)}, u32[]{:S(2)}, u32[]{:S(2)}) %all-to-all-start.2) | async-done | bytes 1179680 | tf_op jit(solution)/shard_map/all_to_all | solution.py:42
  380.5 1.7 reduce_sum.114
  382.3 0.6 maximum_bitcast_fusion
  382.9 1.4 multiply_add_fusion
  384.4 1.9 fusion.12
  (38 shorter events, 0.3 us)
Async XLA Ops:
  7.2 0.8 copy-start.8
  7.2 1.2 copy-start.9
  7.2 10.6 %copy-start.7 = (s32[2304]{0:T(1024)S(1)}, s32[2304]{0:T(1024)}, u32[]{:S(2)}) copy-start(s32[2304]{0:T(1024)} %param.11) | copy-start | bytes 27652
  7.2 11.3 %copy-start.10 = (s32[1,2,64]{2,1,0:T(2,128)S(1)}, s32[1,2,64]{2,1,0:T(2,128)}, u32[]{:S(2)}) copy-start(s32[1,2,64]{2,1,0:T(2,128)} %param.12) | copy-start | bytes 1540
  7.2 11.4 %copy-start.6 = (bf16[1,2,24,4608]{3,2,1,0:T(8,128)(2,1)S(1)}, bf16[1,2,24,4608]{3,2,1,0:T(8,128)(2,1)}, u32[]{:S(2)}) copy-start(bf16[1,2,24,4608]{3,2,1,0:T(8,128)(2,1)} %param.13) | copy-start | bytes 1327108
  7.2 220.8 %all-gather.2.cloned.1.call-start = ((), (), s32[]{:S(2)}) async-start(), calls=%async_computation.9 | async-start | bytes 23887872 | tf_op jit(solution)/shard_map/all_gather | solution.py:108
  9.2 15.5 %all-to-all-start.5 = ((s32[32,1,2]{2,1,0:T(1,128)}), s32[32,1,2]{2,1,0:T(1,128)S(1)}, u32[]{:S(2)}, u32[]{:S(2)}) async-start(s32[32,1,2]{2,1,0:T(1,128)} %bitcast.21), calls=%async_computation.5 | async-start | bytes 32768 | tf_op jit(solution)/shard_map/all_to_all | solution.py:130
  19.0 209.0 %copy-start = (bf16[1,2,64,4608]{3,2,1,0:T(8,128)(2,1)S(1)}, bf16[1,2,64,4608]{3,2,1,0:T(8,128)(2,1)}, u32[]{:S(2)}) copy-start(bf16[1,2,64,4608]{3,2,1,0:T(8,128)(2,1)} %param.9) | copy-start | bytes 3538948
  24.7 11.2 %all-to-all-start.4 = ((s32[32,1,2]{2,1,0:T(1,128)}), s32[32,1,2]{2,1,0:T(1,128)S(1)}, u32[]{:S(2)}, u32[]{:S(2)}) async-start(s32[32,1,2]{2,1,0:T(1,128)} %bitcast.18), calls=%async_computation.4 | async-start | bytes 32768 | tf_op jit(solution)/shard_map/all_to_all | solution.py:130
  35.9 201.2 %all-to-all-start.7 = ((bf16[32,2,4608]{2,1,0:T(2,128)(2,1)}), bf16[32,2,4608]{2,1,0:T(2,128)(2,1)S(1)}, u32[]{:S(2)}, u32[]{:S(2)}) async-start(bf16[32,2,4608]{2,1,0:T(2,128)(2,1)} %reshape.176), calls=%async_computation.7 | async-start | bytes 1179648 | tf_op jit(solution)/shard_map/all_to_all | solution.py:129
  237.1 20.1 %all-to-all-start.6 = ((bf16[32,2,4608]{2,1,0:T(2,128)(2,1)}), bf16[32,2,4608]{2,1,0:T(2,128)(2,1)}, u32[]{:S(2)}, u32[]{:S(2)}) async-start(bf16[32,2,4608]{2,1,0:T(2,128)(2,1)} %reshape.174), calls=%async_computation.6 | async-start | bytes 1179648 | tf_op jit(solution)/shard_map/all_to_all | solution.py:129
  257.8 11.3 %all-to-all-start.1 = ((f32[32,1,128]{2,1,0:T(1,128)}), f32[32,1,128]{2,1,0:T(1,128)S(1)}, u32[]{:S(2)}, u32[]{:S(2)}) async-start(f32[32,1,128]{2,1,0:T(1,128)} %broadcast_in_dim.15), calls=%async_computation.1 | async-start | bytes 32768 | tf_op jit(solution)/shard_map/all_to_all | solution.py:16
  269.7 11.2 %all-to-all-start = ((f32[32,1,128]{2,1,0:T(1,128)}), f32[32,1,128]{2,1,0:T(1,128)S(1)}, u32[]{:S(2)}, u32[]{:S(2)}) async-start(f32[32,1,128]{2,1,0:T(1,128)} %broadcast_in_dim.14), calls=%async_computation | async-start | bytes 32768 | tf_op jit(solution)/shard_map/all_to_all | solution.py:16
  273.8 109.1 %reduce-scatter.2.cloned.1.call-start = ((), (), s32[]{:S(2)}) async-start(), calls=%async_computation.10 | async-start | bytes 5308416 | tf_op jit(solution)/shard_map/reduce_scatter | solution.py:137
  285.0 6.5 %copy-start.2 = (bf16[64,4608]{1,0:T(8,128)(2,1)S(1)}, bf16[64,4608]{1,0:T(8,128)(2,1)}, u32[]{:S(2)}) copy-start(bf16[64,4608]{1,0:T(8,128)(2,1)} %reshape.177) | copy-start | bytes 1769476
  314.1 32.8 %all-to-all-start.3 = ((f32[32,64,144]{2,1,0:T(8,128)}), f32[32,64,144]{2,1,0:T(8,128)S(1)}, u32[]{:S(2)}, u32[]{:S(2)}) async-start(f32[32,64,144]{2,1,0:T(8,128)} %bitcast.67), calls=%async_computation.3 | async-start | bytes 4194304 | tf_op jit(solution)/shard_map/all_to_all | solution.py:42
  346.9 33.6 %all-to-all-start.2 = ((f32[32,64,144]{2,1,0:T(8,128)}), f32[32,64,144]{2,1,0:T(8,128)}, u32[]{:S(2)}, u32[]{:S(2)}) async-start(f32[32,64,144]{2,1,0:T(8,128)} %bitcast.66), calls=%async_computation.2 | async-start | bytes 4194304 | tf_op jit(solution)/shard_map/all_to_all | solution.py:42
  352.0 30.9 %copy-start.3 = (f32[256,576]{0,1:T(8,128)S(1)}, f32[256,576]{0,1:T(8,128)}, u32[]{:S(2)}) copy-start(f32[256,576]{0,1:T(8,128)} %param.16) | copy-start | bytes 1769476
  352.8 31.6 %copy-start.1 = (bf16[2304,576]{0,1:T(8,128)(2,1)S(1)}, bf16[2304,576]{0,1:T(8,128)(2,1)}, u32[]{:S(2)}) copy-start(bf16[2304,576]{0,1:T(8,128)(2,1)} %param.10) | copy-start | bytes 7962628
  384.3 1.9 copy-start.4
  384.3 1.9 copy-start.5
Sparse Core Ops, SparseCore 0:
  9.8 218.1 all-gather.1
  297.2 55.2 reduce-scatter.1
where the time goes:
time: 394 us; the launch traced here: 393 us
  waiting for transfers between devices  246 us (62%)
  matrix products  60.8 us (15%)
  starting transfers between devices  43 us (11%)
  local copies, waits for them, and re-layouts  21.9 us (6%)
  between operations  14.4 us (4%)
  other arithmetic  7.26 us (2%)
    all_gather x1, waiting for transfers between devices, body(): full_table = lax.all_gather(table, 'dp', axis=1, tiled=True)  187 us
    all_to_all x2, waiting for transfers between devices, sent_and_summed(): lax.all_to_all(parts, axis, split_axis=0, concat_axis=0, tiled=True)  36.5 us
    dot_general x2, matrix products, body(): jnp.dot(error, full_table, preferred_element_type=jnp.float32)  23.6 us
    dot_general x2, matrix products, body(): lax.dot_general(states, full_table, (((1,), (1,)), ((), ())), preferred_e...  18.3 us
    reshape x4, local copies, waits for them, and re-layouts, in_blocks(): array.reshape(*shape[:dim], peers, shape[dim] // peers, *shape[dim + 1:])  13.1 us
    all_to_all x2, starting transfers between devices, body(): lax.all_to_all(sent_targets, 'vocab', split_axis=0, concat_axis=0, tiled=...  12.7 us
    all_to_all x2, starting transfers between devices, body(): lax.all_to_all(sent_rows, 'vocab', split_axis=0, concat_axis=0, tiled=True)  12 us
    dot_general x2, matrix products, body(): lax.dot_general(chosen, states, (((0,), (0,)), ((), ())), preferred_eleme...  10.6 us
  transfers between devices with their start and end apart: 10, of which 8 were waited for; matrix products, arithmetic and copies ran while one was open for 18% of the time, Pallas kernels for 0%

commit v1 on v0

v1 whole, which is shorter than its diff:
```python
import jax
import jax.numpy as jnp
from jax import lax
from jax.sharding import PartitionSpec as P

cap_value = 30.0
beta_one = 0.9
beta_two = 0.95
step_count = 10
epsilon = 1e-08
decay_rate = 0.1


def sent_to_all(array, axis):
    peers = lax.axis_size(axis)
    return lax.all_to_all(
        jnp.broadcast_to(array[None], (peers, *array.shape)), axis, 0, 0, tiled=True
    )


def exchanged(parts, axis):
    return lax.all_to_all(parts, axis, split_axis=0, concat_axis=0, tiled=True)


def select_rows(new_mask, new_count):
    ranked = jnp.cumsum(new_mask) - 1
    wanted = (ranked[None, :] == jnp.arange(new_count, dtype=jnp.int32)[:, None]) & (
        new_mask[None, :] == 1
    )
    return wanted.astype(jnp.bfloat16)


def pack_items(rows, owner, slot, shards, capacity):
    onehot = (owner[:, None] == jnp.arange(shards, dtype=jnp.int32)[None, :]).astype(jnp.int32)
    running = jnp.cumsum(onehot, axis=0)
    ranked = jnp.sum(onehot * running, axis=1) - 1
    place = owner * capacity + ranked
    placing = jnp.arange(shards * capacity, dtype=jnp.int32)[:, None] == place[None, :]
    sent = jnp.dot(placing.astype(jnp.bfloat16), rows, preferred_element_type=jnp.float32).astype(
        jnp.bfloat16
    )
    targets = jnp.sum(placing.astype(jnp.int32) * (slot + 1)[None, :], axis=1) - 1
    return (sent.reshape(shards, capacity, rows.shape[1]), targets.reshape(shards, capacity))


def body(
    hidden, table, new_mask, labels, in_grad, item_owner, item_slot, first_moment, second_moment
):
    blocks, span, width = hidden.shape[1:]
    tokens = blocks * span
    new_count = first_moment.shape[0]
    rows, columns = table.shape
    groups = lax.axis_size("dp")
    shards = lax.axis_size("vocab")
    group = lax.axis_index("dp")
    shard = lax.axis_index("vocab")
    piece = width // shards
    total_tokens = groups * tokens
    row_part = rows // groups
    items_here = in_grad.shape[2]
    capacity = max(2, (2 * items_here + shards - 1) // shards)

    own = lax.dynamic_slice(
        hidden[0].reshape(tokens, width), (0, shard * piece), (tokens, piece)
    ).T
    slices = sent_to_all(own, "dp").transpose(1, 0, 2).reshape(piece, total_tokens)
    states = lax.all_gather(slices, "vocab", axis=0, tiled=True)
    label_row = sent_to_all(labels[0].reshape(tokens), "dp").reshape(total_tokens)

    whole = exchanged(table.reshape(groups, row_part, columns), "dp")
    whole = whole.transpose(1, 0, 2).reshape(row_part, width)

    raw = jnp.dot(whole, states, preferred_element_type=jnp.float32)
    squashed = jnp.tanh(raw / cap_value)
    capped = cap_value * squashed
    expd = jnp.exp(capped)
    row_ids = shard * rows + group * row_part + jnp.arange(row_part, dtype=jnp.int32)
    hits = row_ids[:, None] == label_row[None, :]
    local_total = jnp.sum(expd, axis=0)
    local_pick = jnp.sum(jnp.where(hits, capped, 0.0), axis=0)
    weights = (expd * (1.0 - squashed * squashed)).astype(jnp.bfloat16)
    all_weights = lax.all_gather(weights, "dp", axis=0, tiled=True)

    sums = jnp.concatenate([local_total, local_pick]).reshape(-1, tokens)
    sums = sent_to_all(sums, "vocab").sum(axis=0)
    sums = sent_to_all(sums, "dp").sum(axis=0).reshape(2, total_tokens)
    total, picked = sums[0], sums[1]
    loss = lax.dynamic_slice(
        (jnp.log(total) - picked).reshape(groups, tokens), (group, 0), (1, tokens)
    )
    inverse = 1.0 / total
    label_weight = (
        (jnp.exp(picked) - total) * (1.0 - (picked / cap_value) ** 2)
    ).astype(jnp.bfloat16)
    shard_rows = shard * rows + jnp.arange(rows, dtype=jnp.int32)
    error = jnp.where(
        shard_rows[:, None] == label_row[None, :], label_weight[None, :], all_weights
    )

    partial_states = (
        lax.dot_general(
            table, error, (((0,), (0,)), ((), ())), preferred_element_type=jnp.float32
        )
        * inverse[None, :]
    )
    split = shards // groups
    parts = (
        partial_states.reshape(split, columns // split, groups, tokens)
        .transpose(2, 0, 1, 3)
        .reshape(shards, columns // split, tokens)
    )
    d_states = exchanged(parts, "vocab").sum(axis=0).astype(jnp.bfloat16)
    d_states = lax.ppermute(
        d_states,
        ("dp", "vocab"),
        [
            (z * shards + g * split + s, g * shards + z * split + s)
            for z in range(groups)
            for g in range(groups)
            for s in range(split)
        ],
    )
    d_hidden = d_states.T.reshape(1, blocks, span, columns // split)

    sent_rows = []
    sent_targets = []
    for c in range(blocks):
        block_rows, block_targets = pack_items(
            in_grad[0, c], item_owner[0, c, :, 0], item_slot[0, c], shards, capacity
        )
        sent_rows.append(block_rows)
        sent_targets.append(block_targets)
    got_rows = exchanged(jnp.concatenate(sent_rows, axis=1), "vocab")
    got_targets = exchanged(jnp.concatenate(sent_targets, axis=1), "vocab")
    held = shards * blocks * capacity
    got_rows = got_rows.reshape(held, width).T.reshape(groups, columns, held)
    item_rows = exchanged(got_rows, "dp")
    item_targets = sent_to_all(got_targets.reshape(held), "dp")

    select = select_rows(new_mask, new_count)
    params = jnp.dot(select, table, preferred_element_type=jnp.float32)
    chosen = (
        jnp.dot(select, error, preferred_element_type=jnp.float32) * inverse[None, :]
    ).astype(jnp.bfloat16)
    own_states = lax.dynamic_slice(states, (group * columns, 0), (columns, total_tokens))
    grads = lax.dot_general(
        chosen, own_states, (((1,), (1,)), ((), ())), preferred_element_type=jnp.float32
    )
    picking = (
        jnp.arange(new_count, dtype=jnp.int32)[:, None] == item_targets.reshape(1, -1)
    ).astype(jnp.bfloat16)
    grads = grads + lax.dot_general(
        picking,
        item_rows.transpose(1, 0, 2).reshape(columns, groups * held),
        (((1,), (1,)), ((), ())),
        preferred_element_type=jnp.float32,
    )
    first_out = beta_one * first_moment + (1.0 - beta_one) * grads
    second_out = beta_two * second_moment + (1.0 - beta_two) * grads * grads
    update = (
        first_out
        / (1.0 - beta_one**step_count)
        / (jnp.sqrt(second_out / (1.0 - beta_two**step_count)) + epsilon)
        + decay_rate * params
    )
    return (loss.reshape(1, blocks, span), d_hidden, update, first_out, second_out)


def solution(mesh):
    return jax.shard_map(
        body,
        mesh=mesh,
        in_specs=(
            P("dp", None, None, None),
            P("vocab", "dp"),
            P("vocab"),
            P("dp", None, None),
            P("dp", None, "vocab", None),
            P("dp", None, "vocab", None),
            P("dp", None, "vocab"),
            P("vocab", "dp"),
            P("vocab", "dp"),
        ),
        out_specs=(
            P("dp", None, None),
            P("dp", None, None, "vocab"),
            P("vocab", "dp"),
            P("vocab", "dp"),
            P("vocab", "dp"),
        ),
        check_vma=False,
    )
```

time: 394 us -> 303 us (0.77); the launches traced: 393 us -> 298 us
  waiting for transfers between devices: 246 us -> 143 us
  matrix products: 60.8 us -> 28.9 us
  blocking collectives: 0 us -> 19.8 us
  local copies, waits for them, and re-layouts: 21.9 us -> 30.3 us
  starting transfers between devices: 43 us -> 51.1 us
    all_gather x1 -> x2, waiting for transfers between devices: 187 us -> 0.01 us  [the longest x1 0.01 us: body(): states = lax.all_gather(slices, 'vocab', axis=0, tiled=True)]
    all_to_all x6 -> x5, waiting for transfers between devices: 47.7 us -> 124 us  [exchanged(): return lax.all_to_all(parts, axis, split_axis=0, concat_axis=0, tiled=True)]
    dot_general x7 -> x4, matrix products: 58 us -> 24.1 us  [the longest x1 8.64 us: body(): raw = jnp.dot(whole, states, preferred_element_type=jnp.float32)]
    all_to_all x0 -> x1, blocking collectives: none -> 19.8 us  [sent_to_all(): lax.all_to_all(jnp.broadcast_to(array[None], (peers, *array.shape)), axis...]
    all_to_all x2 -> x4, starting transfers between devices: 8.53 us -> 21 us  [sent_to_all(): lax.all_to_all(jnp.broadcast_to(array[None], (peers, *array.shape)), axis...]
    all_to_all x2 -> x4, waiting for transfers between devices: 10.4 us -> 19 us  [sent_to_all(): lax.all_to_all(jnp.broadcast_to(array[None], (peers, *array.shape)), axis...]
    unnamed x22 -> x28, local copies, waits for them, and re-layouts: 0.05 us -> 8.21 us
    reshape x8 -> x5, local copies, waits for them, and re-layouts: 16.4 us -> 9.12 us  [the longest x1 5.59 us: body(): whole = whole.transpose(1, 0, 2).reshape(row_part, width)]
  transfers between devices with their start and end apart: 10 -> 12, of which waited for: 8 -> 8; matrix products, arithmetic and copies ran while one was open for 18% -> 19% of each run, Pallas kernels for 0% -> 0%
where the time goes in v1:
time: 303 us; the launch traced here: 298 us
  waiting for transfers between devices  143 us (47%)
  starting transfers between devices  51.1 us (17%)
  local copies, waits for them, and re-layouts  30.3 us (10%)
  matrix products  28.9 us (10%)
  blocking collectives  19.8 us (7%)
  between operations  14.4 us (5%)
  other arithmetic  10.1 us (3%)
    all_to_all x5, waiting for transfers between devices, exchanged(): return lax.all_to_all(parts, axis, split_axis=0, concat_axis=0, tiled=True)  124 us
    all_to_all x5, starting transfers between devices, exchanged(): return lax.all_to_all(parts, axis, split_axis=0, concat_axis=0, tiled=True)  28.6 us
    all_to_all x4, starting transfers between devices, sent_to_all(): lax.all_to_all(jnp.broadcast_to(array[None], (peers, *array.shape)), axis...  21 us
    all_to_all x1, blocking collectives, sent_to_all(): lax.all_to_all(jnp.broadcast_to(array[None], (peers, *array.shape)), axis...  19.8 us
    all_to_all x4, waiting for transfers between devices, sent_to_all(): lax.all_to_all(jnp.broadcast_to(array[None], (peers, *array.shape)), axis...  19 us
    dot_general x1, matrix products, body(): raw = jnp.dot(whole, states, preferred_element_type=jnp.float32)  8.64 us
    unnamed x28, local copies, waits for them, and re-layouts  8.21 us
    dot_general x1, matrix products, body(): lax.dot_general(table, error, (((0,), (0,)), ((), ())), preferred_element...  6.17 us
  transfers between devices with their start and end apart: 12, of which 8 were waited for; matrix products, arithmetic and copies ran while one was open for 19% of the time, Pallas kernels for 0%

profile of v1, /device:TPU:1, one launch (start us, length us, event | category | flops | bytes accessed | tf_op | source)
XLA Modules:
  0.0 297.9 jit_solution(17045578333989948955)
XLA Ops:
  7.2 1.2 copy-done
  8.5 0.1 copy.67
  8.7 19.8 %all_to_all.56 = bf16[8,144,128]{2,1,0:T(8,128)(2,1)S(1)} all-to-all(bf16[8,144,128]{2,1,0:T(8,128)(2,1)S(1)} %broadcast_in_dim.26), channel_id=1, replica_groups=mesh['dp'=8,'vocab'=32] {'dp'}, dimensions={0} | all-to-all | bytes 589824 | tf_op jit(solution)/shard_map/all_to_all | solution.py:16
  28.5 0.7 copy_bitcast_fusion
  29.2 4.5 %copy.57 = bf16[2304,576]{1,0:T(8,128)(2,1)} copy(bf16[2304,576]{0,1:T(8,128)(2,1)} %param.10) | data formatting | bytes 5308416 | tf_op args[1]
  33.8 4.6 %all-to-all-start.1 = ((bf16[8,288,576]{2,1,0:T(8,128)(2,1)}), bf16[8,288,576]{2,1,0:T(8,128)(2,1)}, u32[]{:S(2)}, u32[]{:S(2)}) async-start(bf16[8,288,576]{2,1,0:T(8,128)(2,1)} %bitcast.81), calls=%async_computation.1 | async-start | bytes 5898240 | tf_op jit(solution)/shard_map/all_to_all | solution.py:22
  38.4 66.0 %all-to-all-done.1 = bf16[8,288,576]{2,1,0:T(8,128)(2,1)} async-done(((bf16[8,288,576]{2,1,0:T(8,128)(2,1)}), bf16[8,288,576]{2,1,0:T(8,128)(2,1)}, u32[]{:S(2)}, u32[]{:S(2)}) %all-to-all-start.1) | async-done | bytes 2654240 | tf_op jit(solution)/shard_map/all_to_all | solution.py:22
  104.4 0.6 broadcast_in_dim.28
  105.0 4.6 %all-to-all-start.2 = ((s32[8,1,128]{2,1,0:T(1,128)}), s32[8,1,128]{2,1,0:T(1,128)S(1)}, u32[]{:S(2)}, u32[]{:S(2)}) async-start(s32[8,1,128]{2,1,0:T(1,128)} %broadcast_in_dim.28), calls=%async_computation.2 | async-start | bytes 8192 | tf_op jit(solution)/shard_map/all_to_all | solution.py:16
  109.7 4.5 %copy.58 = bf16[288,8,576]{2,1,0:T(8,128)(2,1)} copy(bf16[288,8,576]{2,0,1:T(8,128)(2,1)} %bitcast.4) | data formatting | bytes 5308416 | tf_op jit(solution)/shard_map/transpose | solution.py:71
  114.1 5.6 %reshape.195 = bf16[288,4608]{1,0:T(8,128)(2,1)} reshape(bf16[288,8,576]{2,1,0:T(8,128)(2,1)} %copy.58) | data formatting | bytes 5308416 | tf_op jit(solution)/shard_map/reshape | solution.py:71
  119.8 8.6 %fusion.28 = (f32[1024]{0:T(1024)S(1)}, f32[1024]{0:T(1024)S(1)}, bf16[288,1024]{1,0:T(8,128)(2,1)}) fusion(s32[1024]{0:T(1024)S(1)} %bitcast.89, s32[288]{0:T(512)S(1)} %iota_add_fusion.1, bf16[288,4608]{1,0:T(8,128)(2,1)} %reshape.195, bf16[4608,1024]{1,0:T(8,128)(2,1)} %all-gather.3.cloned.1.call-done), kind=kOutput, calls=%fused_computation.29 | convolution fusion | flops 2720856064 | bytes 12694656 | tf_op jit(solution)/shard_map/dot_general | solution.py:73
  128.7 0.2 select_reduce_fusion.1
  129.0 0.1 sub.61
  129.2 0.1 select_reduce_fusion
  129.3 0.1 sub.64
  129.5 0.7 copy.62
  130.2 10.2 %all-to-all-start.6 = ((s32[32,1,4]{2,1,0:T(1,128)}), s32[32,1,4]{2,1,0:T(1,128)S(1)}, u32[]{:S(2)}, u32[]{:S(2)}) async-start(s32[32,1,4]{2,1,0:T(1,128)} %copy.62), calls=%async_computation.6 | async-start | bytes 32768 | tf_op jit(solution)/shard_map/all_to_all | solution.py:22
  140.4 0.4 convolution_convert_fusion.1
  140.8 0.4 convolution_convert_fusion
  141.3 0.2 reshape.202
  141.5 0.2 reshape.203
  141.7 5.6 %all-to-all-done.6 = s32[32,1,4]{2,1,0:T(1,128)S(1)} async-done(((s32[32,1,4]{2,1,0:T(1,128)}), s32[32,1,4]{2,1,0:T(1,128)S(1)}, u32[]{:S(2)}, u32[]{:S(2)}) %all-to-all-start.6) | async-done | bytes 544 | tf_op jit(solution)/shard_map/all_to_all | solution.py:22
  147.3 0.5 broadcast.167
  147.8 0.7 reduce.9
  148.5 0.1 broadcast_in_dim.33
  148.6 0.6 broadcast_in_dim.34
  149.2 6.8 %all-to-all-start.7 = ((s32[8,1,128]{2,1,0:T(1,128)}), s32[8,1,128]{2,1,0:T(1,128)S(1)}, u32[]{:S(2)}, u32[]{:S(2)}) async-start(s32[8,1,128]{2,1,0:T(1,128)} %broadcast_in_dim.34), calls=%async_computation.7 | async-start | bytes 8192 | tf_op jit(solution)/shard_map/all_to_all | solution.py:16
  156.0 6.7 %all-to-all-done.7 = s32[8,1,128]{2,1,0:T(1,128)S(1)} async-done(((s32[8,1,128]{2,1,0:T(1,128)}), s32[8,1,128]{2,1,0:T(1,128)S(1)}, u32[]{:S(2)}, u32[]{:S(2)}) %all-to-all-start.7) | async-done | bytes 4128 | tf_op jit(solution)/shard_map/all_to_all | solution.py:16
  162.7 0.7 broadcast_in_dim.30
  163.4 5.6 %all-to-all-start.3 = ((f32[32,16,128]{2,1,0:T(8,128)}), f32[32,16,128]{2,1,0:T(8,128)S(1)}, u32[]{:S(2)}, u32[]{:S(2)}) async-start(f32[32,16,128]{2,1,0:T(8,128)} %broadcast_in_dim.30), calls=%async_computation.3 | async-start | bytes 524288 | tf_op jit(solution)/shard_map/all_to_all | solution.py:16
  169.1 2.2 pad_maximum_fusion
  171.3 6.8 %all-to-all-done.3 = f32[32,16,128]{2,1,0:T(8,128)S(1)} async-done(((f32[32,16,128]{2,1,0:T(8,128)}), f32[32,16,128]{2,1,0:T(8,128)S(1)}, u32[]{:S(2)}, u32[]{:S(2)}) %all-to-all-start.3) | async-done | bytes 262176 | tf_op jit(solution)/shard_map/all_to_all | solution.py:16
  178.1 3.8 %all-to-all-start.8 = ((bf16[32,4,4608]{2,1,0:T(4,128)(2,1)}), bf16[32,4,4608]{2,1,0:T(4,128)(2,1)S(1)}, u32[]{:S(2)}, u32[]{:S(2)}) async-start(bf16[32,4,4608]{2,1,0:T(4,128)(2,1)} %pad_maximum_fusion), calls=%async_computation.8 | async-start | bytes 2359296 | tf_op jit(solution)/shard_map/all_to_all | solution.py:22
  182.0 18.4 %all-to-all-done.8 = bf16[32,4,4608]{2,1,0:T(4,128)(2,1)S(1)} async-done(((bf16[32,4,4608]{2,1,0:T(4,128)(2,1)}), bf16[32,4,4608]{2,1,0:T(4,128)(2,1)S(1)}, u32[]{:S(2)}, u32[]{:S(2)}) %all-to-all-start.8) | async-done | bytes 1179680 | tf_op jit(solution)/shard_map/all_to_all | solution.py:22
  200.4 0.6 broadcast_in_dim.31
  201.0 4.0 %all-to-all-start.4 = ((f32[8,16,128]{2,1,0:T(8,128)}), f32[8,16,128]{2,1,0:T(8,128)}, u32[]{:S(2)}, u32[]{:S(2)}) async-start(f32[8,16,128]{2,1,0:T(8,128)} %broadcast_in_dim.31), calls=%async_computation.4 | async-start | bytes 131072 | tf_op jit(solution)/shard_map/all_to_all | solution.py:16
  205.0 0.3 reshape.204
  205.3 1.4 copy.63
  206.7 5.5 %all-to-all-done.4 = f32[8,16,128]{2,1,0:T(8,128)} async-done(((f32[8,16,128]{2,1,0:T(8,128)}), f32[8,16,128]{2,1,0:T(8,128)}, u32[]{:S(2)}, u32[]{:S(2)}) %all-to-all-start.4) | async-done | bytes 65568 | tf_op jit(solution)/shard_map/all_to_all | solution.py:16
  212.2 3.7 %all-to-all-start.9 = ((bf16[8,576,128]{2,1,0:T(8,128)(2,1)}), bf16[8,576,128]{2,1,0:T(8,128)(2,1)S(1)}, u32[]{:S(2)}, u32[]{:S(2)}) async-start(bf16[8,576,128]{2,1,0:T(8,128)(2,1)} %bitcast.28), calls=%async_computation.9 | async-start | bytes 2359296 | tf_op jit(solution)/shard_map/all_to_all | solution.py:22
  216.0 0.9 reduce_sum.84
  216.8 0.6 divide_bitcast_fusion
  217.4 6.2 %multiply_bitcast_fusion = f32[72,8,8,128]{3,1,2,0:T(8,128)S(1)} fusion(bf16[2304,576]{0,1:T(8,128)(2,1)} %param.10, bf16[2304,1024]{1,0:T(8,128)(2,1)} %all-gather.5.cloned.1.call-done, s32[1024]{0:T(1024)S(1)} %bitcast.90, s32[2304]{0:T(1024)S(1)} %iota_add_fusion, bf16[1024]{0:T(1024)(128)(2,1)S(1)} %get-tuple-element.26, f32[1024]{0:T(1024)S(1)} %get-tuple-element.25), kind=kOutput, calls=%fused_computation.4 | convolution fusion | flops 2723217408 | bytes 9751552 | tf_op jit(solution)/shard_map/dot_general | solution.py:101
  223.7 0.5 copy.70
  224.2 1.8 copy.59
  226.0 19.6 %all-to-all-done.9 = bf16[8,576,128]{2,1,0:T(8,128)(2,1)S(1)} async-done(((bf16[8,576,128]{2,1,0:T(8,128)(2,1)}), bf16[8,576,128]{2,1,0:T(8,128)(2,1)S(1)}, u32[]{:S(2)}, u32[]{:S(2)}) %all-to-all-start.9) | async-done | bytes 1179680 | tf_op jit(solution)/shard_map/all_to_all | solution.py:22
  245.6 1.0 copy-done.1
  246.6 6.3 %all-to-all-start.5 = ((f32[32,144,128]{2,1,0:T(8,128)}), f32[32,144,128]{2,1,0:T(8,128)S(1)}, u32[]{:S(2)}, u32[]{:S(2)}) async-start(f32[32,144,128]{2,1,0:T(8,128)} %bitcast.14), calls=%async_computation.5 | async-start | bytes 4718592 | tf_op jit(solution)/shard_map/all_to_all | solution.py:22
  253.0 1.0 reduce-window.9
  254.0 0.7 slice.45
  254.6 1.3 reduce-window.12
  256.0 0.8 slice_reduce_fusion
  256.8 1.3 broadcast_compare_fusion
  258.1 0.7 add_bitcast_fusion
  258.8 0.7 fusion.44
  259.5 0.6 reshape.196
  260.1 5.9 %fusion.22 = f32[256,576]{0,1:T(8,128)} fusion(bf16[4608,1024]{1,0:T(8,128)(2,1)} %all-gather.3.cloned.1.call-done, s32[]{:T(128)S(6)} %select_n.21, bf16[2304,1024]{1,0:T(8,128)(2,1)} %all-gather.5.cloned.1.call-done, s32[1024]{0:T(1024)} %bitcast.91, s32[2304]{0:T(1024)} %copy-done.3, bf16[1024]{0:T(1024)(128)(2,1)} %copy-done.9, ...), kind=kOutput, calls=%fused_computation.23 | convolution fusion | flops 1516371968 | bytes 6525956 | tf_op jit(solution)/shard_map/dot_general | solution.py:146
  266.1 3.4 %multiply_add_fusion = (f32[256,576]{0,1:T(8,128)}, f32[256,576]{0,1:T(8,128)}) fusion(f32[256,576]{0,1:T(8,128)} %param.16, f32[256,576]{0,1:T(8,128)} %param.17, f32[256,576]{0,1:T(8,128)} %fusion.22, s32[1024]{0:T(1024)S(1)} %bitcast.88, bf16[8,576,128]{2,1,0:T(8,128)(2,1)} %copy-done.1), kind=kOutput, calls=%fused_computation.33 | convolution fusion | flops 303431680 | bytes 4132864 | tf_op jit(solution)/shard_map/dot_general | solution.py:152
  269.4 14.8 %all-to-all-done.5 = f32[32,144,128]{2,1,0:T(8,128)S(1)} async-done(((f32[32,144,128]{2,1,0:T(8,128)}), f32[32,144,128]{2,1,0:T(8,128)S(1)}, u32[]{:S(2)}, u32[]{:S(2)}) %all-to-all-start.5) | async-done | bytes 2359328 | tf_op jit(solution)/shard_map/all_to_all | solution.py:22
  284.2 0.7 reduce_sum.85
  285.0 1.4 collective-permute-start
  286.4 3.9 %fusion.15 = f32[256,576]{0,1:T(8,128)} fusion(bf16[2304,576]{0,1:T(8,128)(2,1)} %param.10, s32[2304]{0:T(1024)S(1)} %copy-done.4, pred[2304]{0:T(1024)(128)(4,1)S(1)} %copy-done.8, f32[256,576]{0,1:T(8,128)} %get-tuple-element.24, f32[256,576]{0,1:T(8,128)} %get-tuple-element.23), kind=kOutput, calls=%fused_computation.14 | convolution fusion | flops 681541632 | bytes 4435200 | tf_op jit(solution)/shard_map/dot_general | solution.py:141
  290.3 0.7 copy.66
  (50 shorter events, 1.0 us)
Async XLA Ops:
  7.2 1.3 copy-start
  7.2 112.6 %all-gather.3.cloned.1.call-start = ((), (), s32[]{:S(2)}) async-start(), calls=%async_computation.10 | async-start | bytes 9732096 | tf_op jit(solution)/shard_map/all_gather | solution.py:67
  33.8 4.6 %copy-start.11 = (s32[1,2,64]{2,1,0:T(2,128)S(1)}, s32[1,2,64]{2,1,0:T(2,128)}, u32[]{:S(2)}) copy-start(s32[1,2,64]{2,1,0:T(2,128)} %param.12) | copy-start | bytes 1540
  33.8 70.6 %all-to-all-start.1 = ((bf16[8,288,576]{2,1,0:T(8,128)(2,1)}), bf16[8,288,576]{2,1,0:T(8,128)(2,1)}, u32[]{:S(2)}, u32[]{:S(2)}) async-start(bf16[8,288,576]{2,1,0:T(8,128)(2,1)} %bitcast.81), calls=%async_computation.1 | async-start | bytes 5898240 | tf_op jit(solution)/shard_map/all_to_all | solution.py:22
  105.0 14.7 %all-to-all-start.2 = ((s32[8,1,128]{2,1,0:T(1,128)}), s32[8,1,128]{2,1,0:T(1,128)S(1)}, u32[]{:S(2)}, u32[]{:S(2)}) async-start(s32[8,1,128]{2,1,0:T(1,128)} %broadcast_in_dim.28), calls=%async_computation.2 | async-start | bytes 8192 | tf_op jit(solution)/shard_map/all_to_all | solution.py:16
  109.6 107.8 %all-gather.5.cloned.1.call-start = ((), (), s32[]{:S(2)}) async-start(), calls=%async_computation.11 | async-start | bytes 5308416 | tf_op jit(solution)/shard_map/all_gather | solution.py:82
  119.7 97.7 %copy-start.6 = (s32[8,1,128]{2,1,0:T(1,128)}, s32[8,1,128]{2,1,0:T(1,128)S(1)}, u32[]{:S(2)}) copy-start(s32[8,1,128]{2,1,0:T(1,128)S(1)} %all-to-all-done.2) | copy-start | bytes 12292
  119.8 8.7 %copy-start.5 = (s32[1,2,24,1]{2,3,1,0:T(1,128)S(1)}, s32[1,2,24,1]{2,3,1,0:T(1,128)}, u32[]{:S(2)}) copy-start(s32[1,2,24,1]{2,3,1,0:T(1,128)} %param.14) | copy-start | bytes 580
  119.8 9.1 %copy-start.10 = (s32[1,2,24]{2,1,0:T(2,128)S(1)}, s32[1,2,24]{2,1,0:T(2,128)}, u32[]{:S(2)}) copy-start(s32[1,2,24]{2,1,0:T(2,128)} %param.15) | copy-start | bytes 580
  119.8 20.6 %copy-start.2 = (bf16[1,2,24,4608]{3,2,1,0:T(8,128)(2,1)S(1)}, bf16[1,2,24,4608]{3,2,1,0:T(8,128)(2,1)}, u32[]{:S(2)}) copy-start(bf16[1,2,24,4608]{3,2,1,0:T(8,128)(2,1)} %param.13) | copy-start | bytes 1327108
  130.2 17.1 %all-to-all-start.6 = ((s32[32,1,4]{2,1,0:T(1,128)}), s32[32,1,4]{2,1,0:T(1,128)S(1)}, u32[]{:S(2)}, u32[]{:S(2)}) async-start(s32[32,1,4]{2,1,0:T(1,128)} %copy.62), calls=%async_computation.6 | async-start | bytes 32768 | tf_op jit(solution)/shard_map/all_to_all | solution.py:22
  149.2 13.5 %all-to-all-start.7 = ((s32[8,1,128]{2,1,0:T(1,128)}), s32[8,1,128]{2,1,0:T(1,128)S(1)}, u32[]{:S(2)}, u32[]{:S(2)}) async-start(s32[8,1,128]{2,1,0:T(1,128)} %broadcast_in_dim.34), calls=%async_computation.7 | async-start | bytes 8192 | tf_op jit(solution)/shard_map/all_to_all | solution.py:16
  163.4 14.7 %all-to-all-start.3 = ((f32[32,16,128]{2,1,0:T(8,128)}), f32[32,16,128]{2,1,0:T(8,128)S(1)}, u32[]{:S(2)}, u32[]{:S(2)}) async-start(f32[32,16,128]{2,1,0:T(8,128)} %broadcast_in_dim.30), calls=%async_computation.3 | async-start | bytes 524288 | tf_op jit(solution)/shard_map/all_to_all | solution.py:16
  178.1 22.2 %all-to-all-start.8 = ((bf16[32,4,4608]{2,1,0:T(4,128)(2,1)}), bf16[32,4,4608]{2,1,0:T(4,128)(2,1)S(1)}, u32[]{:S(2)}, u32[]{:S(2)}) async-start(bf16[32,4,4608]{2,1,0:T(4,128)(2,1)} %pad_maximum_fusion), calls=%async_computation.8 | async-start | bytes 2359296 | tf_op jit(solution)/shard_map/all_to_all | solution.py:22
  201.0 11.2 %all-to-all-start.4 = ((f32[8,16,128]{2,1,0:T(8,128)}), f32[8,16,128]{2,1,0:T(8,128)}, u32[]{:S(2)}, u32[]{:S(2)}) async-start(f32[8,16,128]{2,1,0:T(8,128)} %broadcast_in_dim.31), calls=%async_computation.4 | async-start | bytes 131072 | tf_op jit(solution)/shard_map/all_to_all | solution.py:16
  212.2 33.4 %all-to-all-start.9 = ((bf16[8,576,128]{2,1,0:T(8,128)(2,1)}), bf16[8,576,128]{2,1,0:T(8,128)(2,1)S(1)}, u32[]{:S(2)}, u32[]{:S(2)}) async-start(bf16[8,576,128]{2,1,0:T(8,128)(2,1)} %bitcast.28), calls=%async_computation.9 | async-start | bytes 2359296 | tf_op jit(solution)/shard_map/all_to_all | solution.py:22
  216.0 7.7 %copy-start.3 = (s32[2304]{0:T(1024)}, s32[2304]{0:T(1024)S(1)}, u32[]{:S(2)}) copy-start(s32[2304]{0:T(1024)S(1)} %iota_add_fusion) | copy-start | bytes 27652
  217.4 6.2 %copy-start.7 = (f32[1024]{0:T(1024)}, f32[1024]{0:T(1024)S(1)}, u32[]{:S(2)}) copy-start(f32[1024]{0:T(1024)S(1)} %get-tuple-element.25) | copy-start | bytes 12292
  217.4 6.2 %copy-start.9 = (bf16[1024]{0:T(1024)(128)(2,1)}, bf16[1024]{0:T(1024)(128)(2,1)S(1)}, u32[]{:S(2)}) copy-start(bf16[1024]{0:T(1024)(128)(2,1)S(1)} %get-tuple-element.26) | copy-start | bytes 6148
  245.6 1.0 copy-start.1
  246.6 37.6 %all-to-all-start.5 = ((f32[32,144,128]{2,1,0:T(8,128)}), f32[32,144,128]{2,1,0:T(8,128)S(1)}, u32[]{:S(2)}, u32[]{:S(2)}) async-start(f32[32,144,128]{2,1,0:T(8,128)} %bitcast.14), calls=%async_computation.5 | async-start | bytes 4718592 | tf_op jit(solution)/shard_map/all_to_all | solution.py:22
  266.1 20.3 %copy-start.4 = (s32[2304]{0:T(1024)S(1)}, s32[2304]{0:T(1024)}, u32[]{:S(2)}) copy-start(s32[2304]{0:T(1024)} %add_bitcast_fusion) | copy-start | bytes 27652
  269.4 17.0 %copy-start.8 = (pred[2304]{0:T(1024)(128)(4,1)S(1)}, pred[2304]{0:T(1024)(128)(4,1)}, u32[]{:S(2)}) copy-start(pred[2304]{0:T(1024)(128)(4,1)} %broadcast_compare_fusion) | copy-start | bytes 6916
  285.0 5.3 %collective-permute-start = (bf16[144,128]{1,0:T(8,128)(2,1)}, bf16[144,128]{1,0:T(8,128)(2,1)S(1)}, u32[]{:S(2)}, u32[]{:S(2)}) collective-permute-start(bf16[144,128]{1,0:T(8,128)(2,1)} %reduce_sum.85), channel_id=1, source_target_pairs={{0,0},{1,1},{2,2},{3,3},{4,32},{5,33},{6,34},{7,35},{8,64},{9,65},... | collective-permute-start | bytes 110600 | tf_op jit(solution)/shard_map/ppermute | solution.py:113
Sparse Core Ops, SparseCore 0:
  29.4 58.7 all-gather.2
  128.6 63.5 all-gather.4
